TPU v7x, 32 devices: a whole 2x2x4 slice. The times are simulated.
32 devices in a mesh: grp: 16 (over z, y, core), dev: 2 (over x).
Axes of the slice: x: 2, y: 2, z: 4, core: 2. Of those that a mesh axis runs over, the one named last changes fastest.
Arguments:
- stack: bfloat16 [608, 128, 512], P('grp', None, 'dev'), may hold values from -12 to 12
- network: int32 [608, 2], replicated, may hold values from 0 to 149, as said below
- bands: int32 [149], replicated, may hold values from 1 to 8
Outputs:
- deramped: bfloat16 [149, 128, 512], P(None, 'grp', 'dev')
- misfit: float32 [128, 512], P('grp', 'dev')
- spectrum: float32 [2, 149, 15, 15], replicated
Inputs may be any that keep to these rules, and one draw needn't show every extreme that they name: `network`: each row holds a reference date and a later secondary date, both below 150; every pair of consecutive dates is some row.
All inputs are finite; a program needn't handle non-finite values.
Results may differ from a plain program's by a relative error of at most 0.005.
Values may be sent and summed in bfloat16 or wider, within the bound.
A program may use at most 128 MiB of HBM per device.

v0:
```python
import math

import jax
import jax.numpy as jnp
from jax import lax
from jax.sharding import PartitionSpec as P

BAND = 8


def build_inverse(network, solved):
    dates = jnp.arange(1, solved + 1, dtype=jnp.int32)
    design = (network[:, 1:2] == dates[None, :]).astype(jnp.float32) - (
        network[:, 0:1] == dates[None, :]
    ).astype(jnp.float32)
    normal = jnp.dot(design.T, design, precision=lax.Precision.HIGHEST)
    factor = jnp.linalg.cholesky(normal)
    pinv = jax.scipy.linalg.cho_solve((factor, True), design.T)
    return (pinv.astype(jnp.bfloat16), design.astype(jnp.bfloat16))


def tables(positions, length, count):
    half = (count + 1) // 2
    steps = jnp.arange(count, dtype=jnp.int32) - (half - 1)
    turns = positions[:, None] * steps[None, :] % length
    angle = turns.astype(jnp.float32) * (2.0 * math.pi / length)
    return (jnp.cos(angle), jnp.sin(angle))


def on_device(stack, network, bands):
    high = lax.Precision.HIGHEST
    solved = bands.shape[0]
    freqs = 2 * BAND - 1
    pinv, design = build_inverse(network, solved)
    block = lax.all_to_all(stack, "grp", split_axis=1, concat_axis=0, tiled=True)
    ifgs, strip, items = block.shape
    flat = block.reshape(ifgs, strip * items)
    series = jnp.dot(pinv, flat, preferred_element_type=jnp.float32)
    model = jnp.dot(design, series.astype(jnp.bfloat16), preferred_element_type=jnp.float32)
    resid = flat.astype(jnp.float32) - model
    fitted = jnp.sqrt(jnp.mean(resid * resid, axis=0) + 1e-06)
    series, fitted = (series.reshape(solved, strip, items), fitted.reshape(1, strip, items))
    row_dev = series.shape[1]
    col_dev = series.shape[2]
    rows_all = row_dev * lax.axis_size("grp")
    cols_all = col_dev * lax.axis_size("dev")
    row_pos = lax.axis_index("grp") * row_dev + jnp.arange(row_dev, dtype=jnp.int32)
    col_pos = lax.axis_index("dev") * col_dev + jnp.arange(col_dev, dtype=jnp.int32)
    row_cos, row_sin = tables(row_pos, rows_all, freqs)
    col_cos, col_sin = tables(col_pos, cols_all, freqs)
    part_cos = jnp.einsum("thw,wl->thl", series, col_cos, precision=high)
    part_sin = jnp.einsum("thw,wl->thl", series, col_sin, precision=high)
    real = jnp.einsum("hk,thl->tkl", row_cos, part_cos, precision=high) - jnp.einsum(
        "hk,thl->tkl", row_sin, part_sin, precision=high
    )
    imag = -(
        jnp.einsum("hk,thl->tkl", row_sin, part_cos, precision=high)
        + jnp.einsum("hk,thl->tkl", row_cos, part_sin, precision=high)
    )
    real, imag = lax.psum((real, imag), ("grp", "dev"))
    scale = 1.0 / (rows_all * cols_all)
    steps = jnp.abs(jnp.arange(freqs, dtype=jnp.int32) - (BAND - 1))
    keep = (steps[None, :] < bands[:, None]).astype(jnp.float32)
    mask = keep[:, :, None] * keep[:, None, :]
    real = real * scale * mask
    imag = imag * scale * mask
    spectrum = jnp.stack([real, imag])
    rising = jnp.einsum("hk,tkl->thl", row_cos, real, precision=high) - jnp.einsum(
        "hk,tkl->thl", row_sin, imag, precision=high
    )
    falling = -(
        jnp.einsum("hk,tkl->thl", row_sin, real, precision=high)
        + jnp.einsum("hk,tkl->thl", row_cos, imag, precision=high)
    )
    ramp = jnp.einsum("thl,wl->thw", rising, col_cos, precision=high) + jnp.einsum(
        "thl,wl->thw", falling, col_sin, precision=high
    )
    deramped = (series - ramp).astype(jnp.bfloat16)
    return (deramped, fitted[0], spectrum)


def solution(mesh):
    return jax.shard_map(
        on_device,
        mesh=mesh,
        in_specs=(P("grp", None, "dev"), P(), P()),
        out_specs=(P(None, "grp", "dev"), P("grp", "dev"), P()),
        check_vma=False,
    )
```

profile of v0, /device:TPU:25, one launch (start us, length us, event | category | flops | bytes accessed | tf_op | source)
XLA Modules:
  0.0 232.1 jit_solution(13909897656060528170)
XLA Ops:
  7.2 4.6 %copy.14 = bf16[38,128,256]{2,0,1:T(8,128)(2,1)} copy(bf16[38,128,256]{2,1,0:T(8,128)(2,1)} %param.3) | data formatting | bytes 4980736 | tf_op args[0]
  11.8 6.5 %all-to-all-start = ((bf16[38,128,256]{2,0,1:T(8,128)(2,1)}), bf16[38,128,256]{2,0,1:T(8,128)(2,1)S(1)}, u32[]{:S(2)}, u32[]{:S(2)}) async-start(bf16[38,128,256]{2,0,1:T(8,128)(2,1)} %copy.14), calls=%async_computation | async-start | bytes 5242880 | tf_op jit(solution)/shard_map/all_to_all | solution.py:35
  18.4 1.5 fusion.11
  19.9 0.1 copy.13
  20.1 11.7 %cholesky.51 = f32[128,128]{1,0:T(8,128)S(1)} custom-call(f32[128,128]{1,0:T(8,128)S(1)} %cholesky.124), custom_call_target="Cholesky" | custom-call | tf_op jit(solution)/shard_map/jit(cholesky)/cholesky | solution.py:17
  31.8 9.8 %custom-call.18 = f32[1,128,128]{1,2,0:T(8,128)S(1)} custom-call(f32[1,128,128]{2,1,0:T(8,128)S(1)} %get-tuple-element.34), custom_call_target="InvertDiagBlocksLowerTriangular" | custom-call | tf_op jit(solution)/shard_map/jit(cholesky)/cholesky | solution.py:17
  41.7 0.2 constant_dynamic-update-slice_fusion.1
  41.8 0.2 convolution_subtract_fusion.3
  42.0 1.9 cholesky.110
  43.9 0.6 compare_reduce_fusion.1
  44.6 0.6 compare_reduce_fusion
  46.6 0.1 fusion.52
  46.7 19.9 %custom-call.19 = f32[2,128,128]{1,2,0:T(8,128)S(1)} custom-call(f32[2,128,128]{2,1,0:T(8,128)S(1)} %pad_maximum_fusion.1), custom_call_target="InvertDiagBlocksLowerTriangular" | custom-call | tf_op jit(solution)/shard_map/jit(_cho_solve)/triangular_solve | solution.py:18
  66.6 0.1 compare_convert_fusion
  66.7 0.1 convert_subtract_fusion.2
  66.8 0.7 fusion.20
  67.5 0.4 convolution_subtract_fusion.2
  68.0 0.3 fusion.64
  68.2 0.2 fusion.150
  68.4 0.7 convolution_subtract_fusion
  69.1 0.5 convolution_convert_fusion
  69.6 3.4 %all-to-all-done = bf16[38,128,256]{2,0,1:T(8,128)(2,1)S(1)} async-done(((bf16[38,128,256]{2,0,1:T(8,128)(2,1)}), bf16[38,128,256]{2,0,1:T(8,128)(2,1)S(1)}, u32[]{:S(2)}, u32[]{:S(2)}) %all-to-all-start) | async-done | bytes 2490400 | tf_op jit(solution)/shard_map/all_to_all | solution.py:35
  73.0 0.6 copy.15
  73.6 0.8 copy.25
  74.4 0.7 fusion.29
  75.1 1.0 multiply_reduce_fusion
  76.1 0.4 copy.26
  76.5 1.2 fusion.5
  77.8 1.2 fusion.7
  79.0 0.4 copy.16
  79.4 0.5 fusion.78
  79.9 0.5 fusion.84
  80.4 0.4 copy.17
  80.8 1.2 fusion.3
  82.0 1.2 fusion.4
  83.3 0.6 sqrt.8
  83.9 129.8 %all-reduce.6.cloned.1.call-done = (f32[149,15,15]{0,1,2:T(8,128)}, f32[149,15,15]{0,1,2:T(8,128)}) async-done(((f32[149,15,15]{0,1,2:T(8,128)}, f32[149,15,15]{0,1,2:T(8,128)}), (f32[149,15,15]{0,1,2:T(8,128)}, f32[149,15,15]{0,1,2:T(8,128)})) %all-reduce.6.cloned.1.call-update) | async-done | bytes 268216 | tf_op jit(solution)/shard_map/psum | solution.py:60
  213.7 1.4 fusion.34
  215.0 1.3 fusion.35
  216.3 1.3 fusion.37
  217.7 0.4 fusion.38
  218.1 1.1 copy.20
  219.3 0.4 copy.22
  219.7 0.4 copy.24
  220.1 0.4 copy.21
  220.5 1.4 copy.23
  222.0 1.2 fusion.15
  223.2 2.1 fusion.1
  (31 shorter events, 0.4 us)
Async XLA Ops:
  11.8 6.5 %copy-start.3 = (s32[608,2]{0,1:T(2,128)S(1)}, s32[608,2]{0,1:T(2,128)}, u32[]{:S(2)}) copy-start(s32[608,2]{0,1:T(2,128)} %param.4) | copy-start | bytes 14596
  11.8 61.2 %all-to-all-start = ((bf16[38,128,256]{2,0,1:T(8,128)(2,1)}), bf16[38,128,256]{2,0,1:T(8,128)(2,1)S(1)}, u32[]{:S(2)}, u32[]{:S(2)}) async-start(bf16[38,128,256]{2,0,1:T(8,128)(2,1)} %copy.14), calls=%async_computation | async-start | bytes 5242880 | tf_op jit(solution)/shard_map/all_to_all | solution.py:35
  18.3 195.4 %all-reduce.6.cloned.1.call-start = ((), (), s32[]{:S(2)}) async-start(), calls=%async_computation.1 | async-start | bytes 983040 | tf_op jit(solution)/shard_map/psum | solution.py:60
  19.9 46.7 %copy-start.4 = (s32[149]{0:T(256)S(1)}, s32[149]{0:T(256)}, u32[]{:S(2)}) copy-start(s32[149]{0:T(256)} %param.5) | copy-start | bytes 1792
  213.7 4.0 %copy-start.2 = (f32[149,15,15]{0,1,2:T(8,128)S(1)}, f32[149,15,15]{0,1,2:T(8,128)}, u32[]{:S(2)}) copy-start(f32[149,15,15]{0,1,2:T(8,128)} %get-tuple-element.32) | copy-start | bytes 402304
  213.7 4.4 %copy-start.1 = (f32[149,15,15]{0,1,2:T(8,128)S(1)}, f32[149,15,15]{0,1,2:T(8,128)}, u32[]{:S(2)}) copy-start(f32[149,15,15]{0,1,2:T(8,128)} %get-tuple-element.31) | copy-start | bytes 402304
  221.9 1.2 copy-start
Sparse Core Ops, SparseCore 0:
  83.4 130.2 all-reduce.5
where the time goes:
time: 236 us; the launch traced here: 232 us
  waiting for transfers between devices  133 us (56%)
  other arithmetic  45.1 us (19%)
  matrix products  19.8 us (8%)
  between operations  15.7 us (7%)
  local copies, waits for them, and re-layouts  11.7 us (5%)
  starting transfers between devices  6.52 us (3%)
    psum x1, waiting for transfers between devices, on_device(): real, imag = lax.psum((real, imag), ('grp', 'dev'))  130 us
    another operation x7, other arithmetic, build_inverse(): factor = jnp.linalg.cholesky(normal)  24.8 us
    another operation x6, other arithmetic, build_inverse(): pinv = jax.scipy.linalg.cho_solve((factor, True), design.T)  20 us
    unnamed x14, local copies, waits for them, and re-layouts  7.01 us
    all_to_all x1, starting transfers between devices, on_device(): lax.all_to_all(stack, 'grp', split_axis=1, concat_axis=0, tiled=True)  6.49 us
  transfers between devices with their start and end apart: 2, of which 2 were waited for; matrix products, arithmetic and copies ran while one was open for 22% of the time, Pallas kernels for 0%

commit v1 on v0

v1 whole, which is shorter than its diff:
```python
import functools
import math

import jax
import jax.numpy as jnp
from jax import lax
from jax.experimental import pallas as pl
from jax.experimental.pallas import tpu as pltpu
from jax.sharding import PartitionSpec as P

BAND = 8
MESH = pl.DeviceIdType.MESH


def build_inverse(network, solved):
    dates = jnp.arange(1, solved + 1, dtype=jnp.int32)
    design = (network[:, 1:2] == dates[None, :]).astype(jnp.float32) - (
        network[:, 0:1] == dates[None, :]
    ).astype(jnp.float32)
    normal = jnp.dot(design.T, design, precision=lax.Precision.HIGHEST)
    factor = jnp.linalg.cholesky(normal)
    pinv = jax.scipy.linalg.cho_solve((factor, True), design.T)
    return (pinv.astype(jnp.bfloat16), design.astype(jnp.bfloat16))


def wave_tables(row_pos, rows_all, col_pos, cols_all):
    lanes = jnp.arange(2 * BAND * BAND, dtype=jnp.int32)
    row_step = lanes // BAND - (BAND - 1)
    col_step = lanes % BAND

    def waves(positions, steps, length):
        turns = positions[:, None] * steps[None, :] % length
        angle = turns.astype(jnp.float32) * (2.0 * math.pi / length)
        return jnp.concatenate([jnp.cos(angle), jnp.sin(angle)], axis=1)

    return waves(row_pos, row_step, rows_all), waves(col_pos, col_step, cols_all)


def basis(row, col):
    half = col.shape[1] // 2
    row_cos, row_sin = row[:, :half], row[:, half:]
    col_cos, col_sin = col[:, :half], col[:, half:]
    cos = row_cos * col_cos - row_sin * col_sin
    sin = row_sin * col_cos + row_cos * col_sin
    return jnp.concatenate([cos, sin], axis=1)


def split(x):
    high = x.astype(jnp.bfloat16)
    return high, (x - high.astype(jnp.float32)).astype(jnp.bfloat16)


def dot3(a, b, dims):
    a_hi, a_lo = split(a)
    b_hi, b_lo = split(b)
    dot = functools.partial(
        lax.dot_general,
        dimension_numbers=(dims, ((), ())),
        preferred_element_type=jnp.float32,
    )
    return dot(a_hi, b_hi) + (dot(a_hi, b_lo) + dot(a_lo, b_hi))


def invert_kernel(per, pinv, design, flat, row_wave, col_wave, series, fitted, parts, acc):
    h = pl.program_id(0)
    data = flat[...]
    out = jnp.dot(pinv[...], data, preferred_element_type=jnp.float32)
    series[...] = out
    model = jnp.dot(design[...], out.astype(jnp.bfloat16), preferred_element_type=jnp.float32)
    resid = data.astype(jnp.float32) - model
    mean = jnp.sum(resid * resid, axis=0, keepdims=True) * (1.0 / data.shape[0])
    fitted[pl.ds(h, 1), :] = jnp.sqrt(mean + 1e-06)
    part = dot3(out, basis(row_wave[pl.ds(h, 1), :], col_wave[...]), ((1,), (0,)))
    solved = part.shape[0]

    @pl.when(h == 0)
    def _():
        acc[...] = jnp.zeros_like(acc)

    acc[0:solved, :] += part

    @pl.when(h == pl.num_programs(0) - 1)
    def _():
        for j in range(parts.shape[0]):
            parts[j] = acc[j * per : (j + 1) * per, :]


def reduce_kernel(n_grp, n_dev, owners, x, y, got, send1, recv1, send2, recv2):
    count = n_grp * n_dev
    me = lax.axis_index("grp") * n_dev + lax.axis_index("dev")

    def coords(d):
        return (d // n_dev, d % n_dev)

    barrier = pltpu.get_barrier_semaphore()

    @pl.loop(1, count)
    def _(t):
        pl.semaphore_signal(
            barrier, inc=1, device_id=coords((me + t) % count), device_id_type=MESH
        )

    pl.semaphore_wait(barrier, count - 1)

    def scatter(dst):
        return pltpu.make_async_remote_copy(
            src_ref=x.at[dst],
            dst_ref=got.at[me],
            send_sem=send1.at[dst],
            recv_sem=recv1.at[me],
            device_id=coords(dst),
            device_id_type=MESH,
        )

    def gather(dst):
        return pltpu.make_async_remote_copy(
            src_ref=y.at[me],
            dst_ref=y.at[me],
            send_sem=send2.at[dst],
            recv_sem=recv2.at[me],
            device_id=coords(dst),
            device_id_type=MESH,
        )

    @pl.loop(1, count)
    def _(t):
        dst = (me + t) % count

        @pl.when(dst < owners)
        def _():
            scatter(dst).start()

    @pl.when(me < owners)
    def _():
        y[me] = x[me]

        @pl.loop(1, count)
        def _(t):
            src = (me + count - t) % count
            pltpu.make_async_remote_copy(
                src_ref=x.at[0],
                dst_ref=got.at[src],
                send_sem=send1.at[src],
                recv_sem=recv1.at[src],
                device_id=coords(src),
                device_id_type=MESH,
            ).wait_recv()
            y[me] += got[src]

        @pl.loop(1, count)
        def _(t):
            gather((me + t) % count).start()

    @pl.loop(1, count)
    def _(t):
        src = (me + count - t) % count

        @pl.when(src < owners)
        def _():
            pltpu.make_async_remote_copy(
                src_ref=y.at[0],
                dst_ref=y.at[src],
                send_sem=send2.at[src],
                recv_sem=recv2.at[src],
                device_id=coords(src),
                device_id_type=MESH,
            ).wait_recv()

    @pl.loop(1, count)
    def _(t):
        dst = (me + t) % count

        @pl.when(dst < owners)
        def _():
            scatter(dst).wait_send()

        @pl.when(me < owners)
        def _():
            gather(dst).wait_send()


def ramp_kernel(scale, coef, bands, series, row_wave, col_wave, deramped, masked, weighted):
    h = pl.program_id(0)

    @pl.when(h == 0)
    def _():
        lane = lax.broadcasted_iota(jnp.int32, coef.shape, 1) % (2 * BAND * BAND)
        row_step = jnp.abs(lane // BAND - (BAND - 1))
        col_step = lane % BAND
        keep = (row_step < bands[...]) & (col_step < bands[...])
        value = jnp.where(keep, coef[...] * scale, 0.0)
        masked[...] = value
        weighted[...] = jnp.where(col_step > 0, value + value, value)

    ramp = dot3(weighted[...], basis(row_wave[pl.ds(h, 1), :], col_wave[...]), ((1,), (1,)))
    deramped[...] = (series[...] - ramp).astype(jnp.bfloat16)


def on_device(stack, network, bands):
    solved = bands.shape[0]
    freqs = 2 * BAND - 1
    lanes = 4 * BAND * BAND
    pinv, design = build_inverse(network, solved)
    block = lax.all_to_all(stack, "grp", split_axis=1, concat_axis=0, tiled=True)
    ifgs, strip, items = block.shape
    flat = block.reshape(ifgs, strip * items)
    n_grp, n_dev = lax.axis_size("grp"), lax.axis_size("dev")
    count = n_grp * n_dev
    per = -(-solved // count)
    owners = -(-solved // per)
    rows_all, cols_all = strip * n_grp, items * n_dev
    row_pos = lax.axis_index("grp") * strip + jnp.arange(strip, dtype=jnp.int32)
    col_pos = lax.axis_index("dev") * items + jnp.arange(items, dtype=jnp.int32)
    row_wave, col_wave = wave_tables(row_pos, rows_all, col_pos, cols_all)

    whole = lambda *shape: pl.BlockSpec(shape, lambda h: (0,) * len(shape))
    tile = lambda rows: pl.BlockSpec((rows, items), lambda h: (0, h))
    series, fitted, parts = pl.pallas_call(
        functools.partial(invert_kernel, per),
        grid=(strip,),
        out_shape=(
            jax.ShapeDtypeStruct((solved, strip * items), jnp.float32),
            jax.ShapeDtypeStruct((strip, items), jnp.float32),
            jax.ShapeDtypeStruct((owners, per, lanes), jnp.float32),
        ),
        in_specs=[
            whole(solved, ifgs),
            whole(ifgs, solved),
            tile(ifgs),
            whole(strip, lanes),
            whole(items, lanes),
        ],
        out_specs=(tile(solved), whole(strip, items), whole(owners, per, lanes)),
        scratch_shapes=[pltpu.VMEM((owners * per, lanes), jnp.float32)],
        name="invert",
    )(pinv, design, flat, row_wave, col_wave)

    vmem = pl.BlockSpec(memory_space=pltpu.VMEM)
    coef = pl.pallas_call(
        functools.partial(reduce_kernel, n_grp, n_dev, owners),
        out_shape=jax.ShapeDtypeStruct((owners, per, lanes), jnp.float32),
        in_specs=[vmem],
        out_specs=vmem,
        scratch_shapes=[
            pltpu.VMEM((count, per, lanes), jnp.float32),
            pltpu.SemaphoreType.DMA((count,)),
            pltpu.SemaphoreType.DMA((count,)),
            pltpu.SemaphoreType.DMA((count,)),
            pltpu.SemaphoreType.DMA((count,)),
        ],
        compiler_params=pltpu.CompilerParams(collective_id=0, has_side_effects=True),
        name="exchange",
    )(parts)
    coef = coef.reshape(owners * per, lanes)[:solved]

    scale = 1.0 / (rows_all * cols_all)
    deramped, masked = pl.pallas_call(
        functools.partial(ramp_kernel, scale),
        grid=(strip,),
        out_shape=(
            jax.ShapeDtypeStruct((solved, strip * items), jnp.bfloat16),
            jax.ShapeDtypeStruct((solved, lanes), jnp.float32),
        ),
        in_specs=[
            whole(solved, lanes),
            whole(solved, 1),
            tile(solved),
            whole(strip, lanes),
            whole(items, lanes),
        ],
        out_specs=(tile(solved), whole(solved, lanes)),
        scratch_shapes=[pltpu.VMEM((solved, lanes), jnp.float32)],
        name="deramp",
    )(coef, bands[:, None], series, row_wave, col_wave)
    half = masked.reshape(solved, 2, 2 * BAND, BAND)[:, :, :freqs, :]
    mirror = half[:, :, ::-1, :0:-1]
    real = jnp.concatenate([mirror[:, 0], half[:, 0]], axis=2)
    imag = jnp.concatenate([mirror[:, 1], -half[:, 1]], axis=2)
    spectrum = jnp.stack([real, imag])
    return (deramped.reshape(solved, strip, items), fitted, spectrum)


def solution(mesh):
    return jax.shard_map(
        on_device,
        mesh=mesh,
        in_specs=(P("grp", None, "dev"), P(), P()),
        out_specs=(P(None, "grp", "dev"), P("grp", "dev"), P()),
        check_vma=False,
    )
```

time: 236 us -> 117 us (0.50); the launches traced: 232 us -> 116 us
  waiting for transfers between devices: 133 us -> 0.01 us
  Pallas kernels: 0 us -> 39.2 us
  matrix products: 19.8 us -> 4.5 us
  between operations: 15.7 us -> 2.23 us
  other arithmetic: 45.1 us -> 48.8 us
  local copies, waits for them, and re-layouts: 11.7 us -> 14.6 us
    psum x1 -> x0, waiting for transfers between devices: 130 us -> none  [on_device(): real, imag = lax.psum((real, imag), ('grp', 'dev'))]
    pallas_call x0 -> x3, Pallas kernels: none -> 39.2 us  [the longest x1 24.5 us: on_device(): pl.pallas_call(functools.partial(reduce_kernel, n_grp, n_dev, owners), ou...]
    dot_general x14 -> x0, matrix products: 15.2 us -> none  [the longest x1 2.06 us: on_device(): jnp.einsum('thl,wl->thw', falling, col_sin, precision=high)]
    all_to_all x1, waiting for transfers between devices: 3.45 us -> 0.01 us  [on_device(): lax.all_to_all(stack, 'grp', split_axis=1, concat_axis=0, tiled=True)]
    dot_general x6 -> x0, local copies, waits for them, and re-layouts: 3.41 us -> none  [the longest x1 1.41 us: on_device(): jnp.einsum('hk,tkl->thl', row_sin, real, precision=high)]
    reshape x0 -> x2, local copies, waits for them, and re-layouts: none -> 2.5 us  [the longest x1 1.64 us: on_device(): coef = coef.reshape(owners * per, lanes)[:solved]]
    unnamed x14 -> x8, local copies, waits for them, and re-layouts: 7.01 us -> 9.23 us
    another operation x6 -> x7, other arithmetic: 20 us -> 20.7 us  [build_inverse(): pinv = jax.scipy.linalg.cho_solve((factor, True), design.T)]
  transfers between devices with their start and end apart: 2 -> 1, of which waited for: 2 -> 0; matrix products, arithmetic and copies ran while one was open for 22% -> 47% of each run, Pallas kernels for 0% -> 0%
where the time goes in v1:
time: 117 us; the launch traced here: 116 us
  other arithmetic  48.8 us (42%)
  Pallas kernels  39.2 us (34%)
  local copies, waits for them, and re-layouts  14.6 us (12%)
  starting transfers between devices  6.49 us (6%)
  matrix products  4.5 us (4%)
  between operations  2.23 us (2%)
    another operation x7, other arithmetic, build_inverse(): factor = jnp.linalg.cholesky(normal)  24.8 us
    pallas_call x1, Pallas kernels, on_device(): pl.pallas_call(functools.partial(reduce_kernel, n_grp, n_dev, owners), ou...  24.5 us
    another operation x7, other arithmetic, build_inverse(): pinv = jax.scipy.linalg.cho_solve((factor, True), design.T)  20.7 us
    unnamed x8, local copies, waits for them, and re-layouts  9.23 us
    pallas_call x1, Pallas kernels, on_device(): pl.pallas_call(functools.partial(invert_kernel, per), grid=(strip,), out_...  8.09 us
    pallas_call x1, Pallas kernels, on_device(): pl.pallas_call(functools.partial(ramp_kernel, scale), grid=(strip,), out_...  6.65 us
    all_to_all x1, starting transfers between devices, on_device(): lax.all_to_all(stack, 'grp', split_axis=1, concat_axis=0, tiled=True)  6.49 us
    another operation x6, matrix products, build_inverse(): pinv = jax.scipy.linalg.cho_solve((factor, True), design.T)  2.65 us
  transfers between devices with their start and end apart: 1, of which 0 were waited for; matrix products, arithmetic and copies ran while one was open for 47% of the time, Pallas kernels for 0%

profile of v1, /device:TPU:25, one launch (start us, length us, event | category | flops | bytes accessed | tf_op | source)
XLA Modules:
  0.0 115.8 jit_solution(13845532331639094798)
XLA Ops:
  0.6 4.6 %copy.28 = bf16[38,128,256]{2,0,1:T(8,128)(2,1)} copy(bf16[38,128,256]{2,1,0:T(8,128)(2,1)} %param.3) | data formatting | bytes 4980736 | tf_op args[0]
  5.2 0.0 copy-start
  5.2 6.5 %all-to-all-start = ((bf16[38,128,256]{2,0,1:T(8,128)(2,1)}), bf16[38,128,256]{2,0,1:T(8,128)(2,1)S(1)}, u32[]{:S(2)}, u32[]{:S(2)}) async-start(bf16[38,128,256]{2,0,1:T(8,128)(2,1)} %copy.28), calls=%async_computation | async-start | bytes 5242880 | tf_op jit(solution)/shard_map/all_to_all | solution.py:204
  11.7 0.0 copy-done
  11.8 1.5 %fusion.1 = f32[149,149]{1,0:T(8,128)S(1)} fusion(s32[149]{0:T(256)S(1)} %iota_add_fusion.1, s32[608]{0:T(1024)S(1)} %get-tuple-element.43, s32[608]{0:T(1024)S(1)} %get-tuple-element.42), kind=kOutput, calls=%fused_computation.6 | convolution fusion | flops 162431456 | bytes 94264 | tf_op jit(solution)/shard_map/dot_general | solution.py:20
  13.3 0.1 copy.26
  13.5 0.0 copy-start.1
  13.5 11.7 %cholesky.52 = f32[128,128]{1,0:T(8,128)S(1)} custom-call(f32[128,128]{1,0:T(8,128)S(1)} %cholesky.127), custom_call_target="Cholesky" | custom-call | tf_op jit(solution)/shard_map/jit(cholesky)/cholesky | solution.py:21
  25.3 9.8 %custom-call.18 = f32[1,128,128]{1,2,0:T(8,128)S(1)} custom-call(f32[1,128,128]{2,1,0:T(8,128)S(1)} %get-tuple-element.49), custom_call_target="InvertDiagBlocksLowerTriangular" | custom-call | tf_op jit(solution)/shard_map/jit(cholesky)/cholesky | solution.py:21
  35.1 0.2 constant_dynamic-update-slice_fusion.1
  35.2 0.1 convolution_subtract_fusion.2
  35.4 1.9 %cholesky.112 = f32[21,21]{1,0:T(8,128)S(1)} custom-call(f32[21,21]{1,0:T(8,128)S(1)} %convolution_subtract_fusion.2), custom_call_target="Cholesky" | custom-call | tf_op jit(solution)/shard_map/jit(cholesky)/cholesky | solution.py:21
  37.3 0.6 compare_reduce_fusion.1
  38.0 0.6 compare_reduce_fusion
  40.0 0.1 fusion.14
  40.1 19.9 %custom-call.19 = f32[2,128,128]{1,2,0:T(8,128)S(1)} custom-call(f32[2,128,128]{2,1,0:T(8,128)S(1)} %pad_maximum_fusion.3), custom_call_target="InvertDiagBlocksLowerTriangular" | custom-call | tf_op jit(solution)/shard_map/jit(_cho_solve)/triangular_solve | solution.py:22
  60.0 0.1 convert_subtract_fusion.2
  60.1 0.7 fusion.4
  60.8 0.4 convolution_subtract_fusion.1
  61.2 0.3 fusion.21
  61.5 0.2 fusion.31
  61.7 0.7 convolution_subtract_fusion
  62.4 0.4 convolution_convert_fusion
  62.8 0.2 copy.27
  63.0 0.0 copy-done.1
  63.0 0.8 copy.30.bands
  63.8 0.1 fusion.28
  63.9 0.6 pad_maximum_fusion.4.row_wave
  64.5 0.7 pad_maximum_fusion.2.pinv
  65.2 0.6 fusion.18
  65.8 0.7 pad_maximum_fusion.1.col_wave
  66.5 0.9 fusion.design
  67.5 0.0 all-to-all-done
  67.5 0.6 copy.29
  68.0 2.3 %copy.33 = bf16[76,8,8,256]{3,1,2,0:T(8,128)(2,1)} copy(bf16[76,8,8,256]{3,2,1,0:T(8,128)(2,1)S(1)} %bitcast.55) | data formatting | bytes 4980736
  70.3 8.1 %invert.1 = (f32[149,2048]{1,0:T(8,128)}, f32[8,256]{1,0:T(8,128)}, f32[30,5,256]{2,1,0:T(8,128)}) custom-call(bf16[149,608]{1,0:T(8,128)(2,1)} %pad_maximum_fusion.2.pinv, bf16[608,149]{1,0:T(8,128)(2,1)} %fusion.design, bf16[608,2048]{1,0:T(8,128)(2,1)} %bitcast.54, f32[8,256]{1,0:T(8,128)} %pad_maximum_fusion.4.row_wave, ...), custom_call_target="tpu_custom_call" | custom-call | tf_op jit(solution)/shard_map/invert/pallas_call | solution.py:218
  78.4 24.5 %exchange.1 = f32[30,5,256]{2,1,0:T(8,128)} custom-call(f32[30,5,256]{2,1,0:T(8,128)} %get-tuple-element.8.x), custom_call_target="tpu_custom_call" | custom-call | tf_op jit(solution)/shard_map/exchange/pallas_call | solution.py:239
  102.9 1.6 %reshape.88 = f32[150,256]{1,0:T(8,128)} reshape(f32[30,5,256]{2,1,0:T(8,128)} %exchange.1) | data formatting | bytes 307200 | tf_op jit(solution)/shard_map/reshape | solution.py:254
  104.5 6.7 %deramp.1 = (bf16[149,2048]{1,0:T(8,128)(2,1)}, f32[149,256]{1,0:T(8,128)}) custom-call(f32[149,256]{1,0:T(8,128)} %bitcast.60, s32[149,1]{1,0:T(8,128)} %copy.30.bands, f32[149,2048]{1,0:T(8,128)} %get-tuple-element.9.series, f32[8,256]{1,0:T(8,128)} %pad_maximum_fusion.4.row_wave, f32[256,256]{1,0:T(8,128)} %pad_maximum_fusion.1.col_wave), custom_call_target="tpu_custom_call" | custom-call | tf_op jit(solution)/shard_map/deramp/pallas_call | solution.py:257
  111.2 1.0 copy.31
  112.3 1.2 %copy.34 = bf16[19,8,8,256]{3,2,1,0:T(8,128)(2,1)S(1)} copy(bf16[19,8,8,256]{3,1,2,0:T(8,128)(2,1)} %bitcast.59) | data formatting | bytes 1245184
  113.5 0.9 slice.134
  114.4 0.1 slice.109
  114.5 0.1 slice.106
  114.7 1.1 copy.32
  (21 shorter events, 0.4 us)
Async XLA Ops:
  5.2 6.5 %copy-start = (s32[608,2]{0,1:T(2,128)S(1)}, s32[608,2]{0,1:T(2,128)}, u32[]{:S(2)}) copy-start(s32[608,2]{0,1:T(2,128)} %param.4) | copy-start | bytes 14596
  5.2 62.2 %all-to-all-start = ((bf16[38,128,256]{2,0,1:T(8,128)(2,1)}), bf16[38,128,256]{2,0,1:T(8,128)(2,1)S(1)}, u32[]{:S(2)}, u32[]{:S(2)}) async-start(bf16[38,128,256]{2,0,1:T(8,128)(2,1)} %copy.28), calls=%async_computation | async-start | bytes 5242880 | tf_op jit(solution)/shard_map/all_to_all | solution.py:204
  13.5 49.5 %copy-start.1 = (s32[149]{0:T(256)S(1)}, s32[149]{0:T(256)}, u32[]{:S(2)}) copy-start(s32[149]{0:T(256)} %param.5) | copy-start | bytes 1792

commit v2 on v1

v2 whole, which is shorter than its diff:
```python
import functools
import math

import jax
import jax.numpy as jnp
import numpy as np
from jax import lax
from jax.experimental import pallas as pl
from jax.experimental.pallas import tpu as pltpu
from jax.sharding import PartitionSpec as P

BAND = 8
LANES = 128
MESH = pl.DeviceIdType.MESH


def wave_tables(row_pos, rows_all, col_pos, cols_all):
    lanes = jnp.arange(2 * BAND * BAND, dtype=jnp.int32)
    row_step = lanes // BAND - (BAND - 1)
    col_step = lanes % BAND

    def waves(positions, steps, length):
        turns = positions[:, None] * steps[None, :] % length
        angle = turns.astype(jnp.float32) * (2.0 * math.pi / length)
        return jnp.concatenate([jnp.cos(angle), jnp.sin(angle)], axis=1)

    return waves(row_pos, row_step, rows_all), waves(col_pos, col_step, cols_all)


def basis(row, col):
    half = col.shape[1] // 2
    row_cos, row_sin = row[:, :half], row[:, half:]
    col_cos, col_sin = col[:, :half], col[:, half:]
    cos = row_cos * col_cos - row_sin * col_sin
    sin = row_sin * col_cos + row_cos * col_sin
    return jnp.concatenate([cos, sin], axis=1)


def split(x):
    high = x.astype(jnp.bfloat16)
    return high, (x - high.astype(jnp.float32)).astype(jnp.bfloat16)


def dot3(a, b, dims):
    a_hi, a_lo = split(a)
    b_hi, b_lo = split(b)
    dot = functools.partial(
        lax.dot_general,
        dimension_numbers=(dims, ((), ())),
        preferred_element_type=jnp.float32,
    )
    return dot(a_hi, b_hi) + (dot(a_hi, b_lo) + dot(a_lo, b_hi))


def split3(x):
    high, rest = split(x)
    low, last = split(x - high.astype(jnp.float32))
    return high, low, last


def sweep(matrix, b):
    rows, lanes = matrix.shape
    lane = lax.broadcasted_iota(jnp.int32, (8, lanes), 1)
    sub = lax.broadcasted_iota(jnp.int32, (8, lanes), 0)
    panel = matrix[pl.ds(pl.multiple_of(b * 8, 8), 8), :]
    work = pltpu.roll(panel, lanes - b * 8, axis=1)
    for r in range(8):
        inv = 1.0 / work[r : r + 1, r : r + 1]
        row = jnp.where(lane[:1] == r, 1.0, work[r : r + 1, :]) * inv
        rest = jnp.where(lane == r, 0.0, work) - work[:, r : r + 1] * row
        work = jnp.where(sub == r, row, rest)
    work = pltpu.roll(work, b * 8, axis=1)
    inside = lane // 8 == b
    unit = jnp.where(lane == sub + b * 8, 1.0, 0.0)
    zero = jnp.where(inside, 0.0, work)
    left = jnp.concatenate([jnp.where(inside, 0.0, -panel), zero, unit], axis=0)
    right = jnp.concatenate([zero, unit, jnp.where(inside, -work, work)], axis=0)
    change = lax.dot_general(
        left[:, :rows],
        right,
        (((0,), (0,)), ((), ())),
        preferred_element_type=jnp.float32,
        precision=lax.Precision.HIGHEST,
    )
    row_of = lax.broadcasted_iota(jnp.int32, (rows, lanes), 0) // 8
    lane_of = lax.broadcasted_iota(jnp.int32, (rows, lanes), 1) // 8
    matrix[...] = jnp.where((row_of == b) | (lane_of == b), 0.0, matrix[...]) + change


def inverse(solved, network, design_t, matrix, pinv):
    rows, lanes = matrix.shape
    date = lax.broadcasted_iota(jnp.int32, design_t.shape, 0) + 1
    one = lambda k: jnp.where(network[k : k + 1, :] == date, 1.0, 0.0)
    design_t[...] = (one(1) - one(0)).astype(jnp.bfloat16)
    normal = lax.dot_general(
        design_t[...],
        design_t[...],
        (((1,), (1,)), ((), ())),
        preferred_element_type=jnp.float32,
    )[:rows]
    row = lax.broadcasted_iota(jnp.int32, (rows, lanes), 0)
    lane = lax.broadcasted_iota(jnp.int32, (rows, lanes), 1)
    matrix[...] = jnp.where((row == lane) & (row >= solved), 1.0, normal)

    @pl.loop(0, rows // 8)
    def _(b):
        sweep(matrix, b)

    total = None
    for piece in split3(-matrix[...]):
        term = jnp.dot(piece, design_t[...], preferred_element_type=jnp.float32)
        total = term if total is None else total + term
    pinv[...] = total.astype(jnp.bfloat16)


def kernel(
    n_grp, n_dev, solved, scale,
    stack, network, bands, row_wave, col_wave, choose,
    deramped, fitted, spectrum,
    block, data, design_t, matrix, pinv, series, acc, x, y, got, coef, flat,
    send0, recv0, own, send1, recv1, send2, recv2,
):
    count = n_grp * n_dev
    grp, dev = lax.axis_index("grp"), lax.axis_index("dev")
    me = grp * n_dev + dev
    ifgs, strip, items = block.shape
    share = stack.shape[0]
    owners, per, lanes = x.shape

    def coords(d):
        return (d // n_dev, d % n_dev)

    barrier = pltpu.get_barrier_semaphore()

    @pl.loop(1, count)
    def _(t):
        pl.semaphore_signal(
            barrier, inc=1, device_id=coords((me + t) % count), device_id_type=MESH
        )

    pl.semaphore_wait(barrier, count - 1)

    def trade(to, slot, place):
        return pltpu.make_async_remote_copy(
            src_ref=stack.at[:, pl.ds(pl.multiple_of(to * strip, strip), strip), :],
            dst_ref=block.at[pl.ds(place * share, share)],
            send_sem=send0.at[to],
            recv_sem=recv0.at[slot],
            device_id=(to, dev),
            device_id_type=MESH,
        )

    @pl.loop(1, n_grp)
    def _(t):
        trade((grp + t) % n_grp, grp, grp).start()

    local = pltpu.make_async_copy(
        stack.at[:, pl.ds(pl.multiple_of(grp * strip, strip), strip), :],
        block.at[pl.ds(grp * share, share)],
        own,
    )
    local.start()

    inverse(solved, network, design_t, matrix, pinv)

    def widen(src):
        piece = block[pl.ds(src * share, share)].astype(jnp.float32)
        start = pl.multiple_of(src * share * strip, strip)
        piece = piece.reshape(share * strip, items)
        for c in range(items // LANES):
            data[c, pl.ds(start, share * strip), :] = piece[:, c * LANES : (c + 1) * LANES]

    local.wait()
    widen(grp)

    @pl.loop(1, n_grp)
    def _(t):
        src = (grp + n_grp - t) % n_grp
        trade(src, src, src).wait_recv()
        widen(src)

    acc[...] = jnp.zeros_like(acc)

    @pl.loop(0, strip)
    def _(h):
        phase = jnp.concatenate(
            [data[c, pl.ds(h, ifgs, stride=strip), :] for c in range(items // LANES)], axis=1
        )
        out = jnp.dot(pinv[...], phase.astype(jnp.bfloat16), preferred_element_type=jnp.float32)
        series[h] = out
        model = lax.dot_general(
            design_t[0 : out.shape[0], :],
            out.astype(jnp.bfloat16),
            (((0,), (0,)), ((), ())),
            preferred_element_type=jnp.float32,
        )
        resid = phase - model
        mean = jnp.sum(resid * resid, axis=0, keepdims=True) * (1.0 / ifgs)
        fitted[pl.ds(h, 1), :] = jnp.sqrt(mean + 1e-06)
        acc[...] += dot3(out, basis(row_wave[pl.ds(h, 1), :], col_wave[...]), ((1,), (0,)))

    for j in range(owners):
        x[j] = acc[j * per : (j + 1) * per, :]

    def scatter(dst):
        return pltpu.make_async_remote_copy(
            src_ref=x.at[dst],
            dst_ref=got.at[me],
            send_sem=send1.at[dst],
            recv_sem=recv1.at[me],
            device_id=coords(dst),
            device_id_type=MESH,
        )

    def gather(dst):
        return pltpu.make_async_remote_copy(
            src_ref=y.at[me],
            dst_ref=y.at[me],
            send_sem=send2.at[dst],
            recv_sem=recv2.at[me],
            device_id=coords(dst),
            device_id_type=MESH,
        )

    @pl.loop(1, count)
    def _(t):
        dst = (me + t) % count

        @pl.when(dst < owners)
        def _():
            scatter(dst).start()

    @pl.when(me < owners)
    def _():
        y[me] = x[me]

        @pl.loop(1, count)
        def _(t):
            src = (me + count - t) % count
            pltpu.make_async_remote_copy(
                src_ref=x.at[0],
                dst_ref=got.at[src],
                send_sem=send1.at[src],
                recv_sem=recv1.at[src],
                device_id=coords(src),
                device_id_type=MESH,
            ).wait_recv()
            y[me] += got[src]

        @pl.loop(1, count)
        def _(t):
            gather((me + t) % count).start()

    @pl.loop(1, count)
    def _(t):
        src = (me + count - t) % count

        @pl.when(src < owners)
        def _():
            pltpu.make_async_remote_copy(
                src_ref=y.at[0],
                dst_ref=y.at[src],
                send_sem=send2.at[src],
                recv_sem=recv2.at[src],
                device_id=coords(src),
                device_id_type=MESH,
            ).wait_recv()

    coef[...] = jnp.zeros_like(coef)
    for j in range(owners):
        coef[j * per : (j + 1) * per, :] = y[j]

    lane = lax.broadcasted_iota(jnp.int32, coef.shape, 1) % (2 * BAND * BAND)
    row_step = jnp.abs(lane // BAND - (BAND - 1))
    col_step = lane % BAND
    keep = (row_step < bands[...]) & (col_step < bands[...])
    value = jnp.where(keep, coef[...] * scale, 0.0)
    coef[...] = jnp.where(col_step > 0, value + value, value)
    total = None
    for piece in split3(value):
        term = lax.dot_general(
            choose[...], piece, (((1,), (1,)), ((), ())), preferred_element_type=jnp.float32
        )
        total = term if total is None else total + term
    spectrum[...] = total[:, :solved]

    @pl.loop(0, strip)
    def _(h):
        ramp = dot3(coef[...], basis(row_wave[pl.ds(h, 1), :], col_wave[...]), ((1,), (1,)))
        rest = series[h] - ramp
        for c in range(items // LANES):
            piece = rest[:, c * LANES : (c + 1) * LANES]
            flat[c, pl.ds(h, coef.shape[0], stride=strip), :] = piece

    for c in range(items // LANES):
        piece = flat[c, 0 : solved * strip, :].reshape(solved, strip, LANES)
        deramped[:, :, c * LANES : (c + 1) * LANES] = piece.astype(jnp.bfloat16)

    @pl.loop(1, n_grp)
    def _(t):
        trade((grp + t) % n_grp, grp, grp).wait_send()

    @pl.loop(1, count)
    def _(t):
        dst = (me + t) % count

        @pl.when(dst < owners)
        def _():
            scatter(dst).wait_send()

        @pl.when(me < owners)
        def _():
            gather(dst).wait_send()


def choice():
    freqs = 2 * BAND - 1
    half = 2 * BAND * BAND
    table = np.zeros((freqs, freqs, 2, 2 * half), np.float32)
    for k in range(freqs):
        for m in range(freqs):
            if m >= BAND - 1:
                at, sign = k * BAND + m - (BAND - 1), -1.0
            else:
                at, sign = (freqs - 1 - k) * BAND + (BAND - 1) - m, 1.0
            table[k, m, 0, at] = 1.0
            table[k, m, 1, half + at] = sign
    return jnp.asarray(table.reshape(-1, 2 * half), jnp.bfloat16)


def on_device(stack, network, bands):
    solved = bands.shape[0]
    freqs = 2 * BAND - 1
    lanes = 4 * BAND * BAND
    n_grp, n_dev = lax.axis_size("grp"), lax.axis_size("dev")
    count = n_grp * n_dev
    share, rows_all, items = stack.shape
    ifgs, strip = share * n_grp, rows_all // n_grp
    cols_all = items * n_dev
    per = -(-solved // count)
    owners = -(-solved // per)
    tall = -(-max(solved, owners * per) // 8) * 8
    wide = -(-tall // 128) * 128
    row_pos = lax.axis_index("grp") * strip + jnp.arange(strip, dtype=jnp.int32)
    col_pos = lax.axis_index("dev") * items + jnp.arange(items, dtype=jnp.int32)
    row_wave, col_wave = wave_tables(row_pos, rows_all, col_pos, cols_all)
    bands = jnp.pad(bands, (0, tall - solved))[:, None]

    vmem = pl.BlockSpec(memory_space=pltpu.VMEM)
    f32, bf16 = jnp.float32, jnp.bfloat16
    sems = lambda n: pltpu.SemaphoreType.DMA((n,))
    deramped, fitted, spectrum = pl.pallas_call(
        functools.partial(kernel, n_grp, n_dev, solved, 1.0 / (rows_all * cols_all)),
        out_shape=(
            jax.ShapeDtypeStruct((solved, strip, items), bf16),
            jax.ShapeDtypeStruct((strip, items), f32),
            jax.ShapeDtypeStruct((2 * freqs * freqs, solved), f32),
        ),
        in_specs=[pl.BlockSpec(memory_space=pl.ANY)] + [vmem] * 5,
        out_specs=(vmem, vmem, vmem),
        scratch_shapes=[
            pltpu.VMEM((ifgs, strip, items), bf16),
            pltpu.VMEM((items // LANES, ifgs * strip, LANES), f32),
            pltpu.VMEM((wide, ifgs), bf16),
            pltpu.VMEM((tall, wide), f32),
            pltpu.VMEM((tall, ifgs), bf16),
            pltpu.VMEM((strip, tall, items), f32),
            pltpu.VMEM((tall, lanes), f32),
            pltpu.VMEM((owners, per, lanes), f32),
            pltpu.VMEM((owners, per, lanes), f32),
            pltpu.VMEM((count, per, lanes), f32),
            pltpu.VMEM((tall, lanes), f32),
            pltpu.VMEM((items // LANES, tall * strip, LANES), f32),
            sems(n_grp),
            sems(n_grp),
            pltpu.SemaphoreType.DMA,
            sems(count),
            sems(count),
            sems(count),
            sems(count),
        ],
        compiler_params=pltpu.CompilerParams(collective_id=0, has_side_effects=True),
        name="whole",
    )(stack, network.T, bands, row_wave, col_wave, choice())
    spectrum = spectrum.reshape(freqs, freqs, 2, solved).transpose(2, 3, 0, 1)
    return (deramped, fitted, spectrum)


def solution(mesh):
    return jax.shard_map(
        on_device,
        mesh=mesh,
        in_specs=(P("grp", None, "dev"), P(), P()),
        out_specs=(P(None, "grp", "dev"), P("grp", "dev"), P()),
        check_vma=False,
    )
```

time: 117 us -> 97.7 us (0.84)
  Pallas kernels: 39.2 us -> 88 us
  other arithmetic: 48.8 us -> 2.05 us
  local copies, waits for them, and re-layouts: 14.6 us -> 6.72 us
  starting transfers between devices: 6.49 us -> 0 us
  matrix products: 4.5 us -> 0 us
  between operations: 2.23 us -> 0.68 us
    pallas_call x3 -> x1, Pallas kernels: 39.2 us -> 88 us  [on_device(): pl.pallas_call(functools.partial(kernel, n_grp, n_dev, solved, 1.0 / (row...]
    another operation x17 -> x0, other arithmetic: 45.6 us -> none  [the longest x7 24.8 us: build_inverse(): factor = jnp.linalg.cholesky(normal)]
    all_to_all x1 -> x0, starting transfers between devices: 6.49 us -> none  [on_device(): lax.all_to_all(stack, 'grp', split_axis=1, concat_axis=0, tiled=True)]
    unnamed x8 -> x2, local copies, waits for them, and re-layouts: 9.23 us -> 3.23 us
    another operation x8 -> x0, matrix products: 2.96 us -> none  [the longest x6 2.65 us: build_inverse(): pinv = jax.scipy.linalg.cho_solve((factor, True), design.T)]
    dot_general x1 -> x0, matrix products: 1.54 us -> none  [build_inverse(): normal = jnp.dot(design.T, design, precision=lax.Precision.HIGHEST)]
    reshape x2 -> x1, local copies, waits for them, and re-layouts: 2.5 us -> 2.06 us  [on_device(): spectrum = spectrum.reshape(freqs, freqs, 2, solved).transpose(2, 3, 0, 1)]
  transfers between devices with their start and end apart: 1 -> 0, of which waited for: 0 -> 0; matrix products, arithmetic and copies ran while one was open for 47% -> 0% of each run, Pallas kernels for 0% -> 0%
where the time goes in v2:
time: 97.7 us; the launch traced here: 97.5 us
  Pallas kernels  88 us (90%)
  local copies, waits for them, and re-layouts  6.72 us (7%)
  other arithmetic  2.05 us (2%)
    pallas_call x1, Pallas kernels, on_device(): pl.pallas_call(functools.partial(kernel, n_grp, n_dev, solved, 1.0 / (row...  88 us
    unnamed x2, local copies, waits for them, and re-layouts  3.23 us
    reshape x1, local copies, waits for them, and re-layouts, on_device(): spectrum = spectrum.reshape(freqs, freqs, 2, solved).transpose(2, 3, 0, 1)  2.06 us

profile of v2, /device:TPU:25, one launch (start us, length us, event | category | flops | bytes accessed | tf_op | source)
XLA Modules:
  0.0 97.5 jit_solution(14513879438851504572)
XLA Ops:
  0.7 0.7 pad.4
  1.4 0.1 fusion.9
  1.5 0.6 pad_maximum_fusion.1.row_wave
  2.1 0.8 copy.7.bands
  2.8 0.6 fusion.4
  3.4 0.7 pad_maximum_fusion.col_wave
  4.2 88.0 %whole.1 = (bf16[149,8,256]{2,1,0:T(8,128)(2,1)}, f32[8,256]{1,0:T(8,128)}, f32[450,149]{1,0:T(8,128)}) custom-call(bf16[38,128,256]{2,1,0:T(8,128)(2,1)} %stack.1, s32[2,608]{1,0:T(2,128)} %bitcast.4, s32[152,1]{1,0:T(8,128)} %copy.7.bands, f32[8,256]{1,0:T(8,128)} %pad_maximum_fusion.1.row_wave, f32[256,256]{1,0:T(8,128)} %pad_maximum_fusion.col_wave, ...), custom_call_target="tpu_custom_call" | custom-call | tf_op jit(solution)/shard_map/whole/pallas_call | solution.py:352
  92.2 2.1 %reshape.40 = f32[15,15,2,149]{3,2,1,0:T(2,128)} reshape(f32[450,149]{1,0:T(8,128)} %get-tuple-element.8) | data formatting | bytes 536400 | tf_op jit(solution)/shard_map/reshape | solution.py:385
  94.2 1.9 %copy.10 = bf16[149,8,256]{2,1,0:T(8,128)(2,1)} copy(bf16[149,8,256]{2,1,0:T(8,128)(2,1)} %get-tuple-element.16) | data formatting | bytes 1220608
  96.2 1.3 %copy.11 = f32[8,256]{1,0:T(8,128)} copy(f32[8,256]{1,0:T(8,128)} %get-tuple-element.17) | data formatting | bytes 16384
  (4 shorter events, 0.0 us)

commit v3 on v2

--- a/solution.py
+++ b/solution.py
@@ -14,26 +14,10 @@
 MESH = pl.DeviceIdType.MESH
 
 
-def wave_tables(row_pos, rows_all, col_pos, cols_all):
-    lanes = jnp.arange(2 * BAND * BAND, dtype=jnp.int32)
-    row_step = lanes // BAND - (BAND - 1)
-    col_step = lanes % BAND
-
-    def waves(positions, steps, length):
-        turns = positions[:, None] * steps[None, :] % length
-        angle = turns.astype(jnp.float32) * (2.0 * math.pi / length)
-        return jnp.concatenate([jnp.cos(angle), jnp.sin(angle)], axis=1)
-
-    return waves(row_pos, row_step, rows_all), waves(col_pos, col_step, cols_all)
-
-
-def basis(row, col):
-    half = col.shape[1] // 2
-    row_cos, row_sin = row[:, :half], row[:, half:]
-    col_cos, col_sin = col[:, :half], col[:, half:]
-    cos = row_cos * col_cos - row_sin * col_sin
-    sin = row_sin * col_cos + row_cos * col_sin
-    return jnp.concatenate([cos, sin], axis=1)
+def waves(start, shape, step, length):
+    position = start + lax.broadcasted_iota(jnp.int32, shape, 0)
+    angle = (position * step % length).astype(jnp.float32) * (2.0 * math.pi / length)
+    return jnp.cos(angle), jnp.sin(angle)
 
 
 def split(x):
@@ -42,8 +26,7 @@
 
 
 def dot3(a, b, dims):
-    a_hi, a_lo = split(a)
-    b_hi, b_lo = split(b)
+    (a_hi, a_lo), (b_hi, b_lo) = a, b
     dot = functools.partial(
         lax.dot_general,
         dimension_numbers=(dims, ((), ())),
@@ -115,9 +98,9 @@
 
 def kernel(
     n_grp, n_dev, solved, scale,
-    stack, network, bands, row_wave, col_wave, choose,
+    stack, network, bands, choose,
     deramped, fitted, spectrum,
-    block, data, design_t, matrix, pinv, series, acc, x, y, got, coef, flat,
+    block, data, design_t, matrix, pinv, series, acc, x, y, got, coef, flat, row_wave, high, low, fit,
     send0, recv0, own, send1, recv1, send2, recv2,
 ):
     count = n_grp * n_dev
@@ -126,6 +109,10 @@
     ifgs, strip, items = block.shape
     share = stack.shape[0]
     owners, per, lanes = x.shape
+    tall = coef.shape[0]
+    pieces, half = items // LANES, lanes // 2
+    pairs = strip // 2
+    rows_all, cols_all = strip * n_grp, items * n_dev
 
     def coords(d):
         return (d // n_dev, d % n_dev)
@@ -140,64 +127,99 @@
 
     pl.semaphore_wait(barrier, count - 1)
 
-    def trade(to, slot, place):
+    def part(ref, c, start, rows, strips=None):
+        cols = pl.ds(c * LANES, LANES)
+        if strips is None:
+            return ref.at[pl.ds(start, rows), :, cols]
+        return ref.at[:, pl.ds(pl.multiple_of(strips * strip, strip), strip), cols]
+
+    def trade(c, to, slot, place):
         return pltpu.make_async_remote_copy(
-            src_ref=stack.at[:, pl.ds(pl.multiple_of(to * strip, strip), strip), :],
-            dst_ref=block.at[pl.ds(place * share, share)],
-            send_sem=send0.at[to],
-            recv_sem=recv0.at[slot],
+            src_ref=part(stack, c, 0, share, to),
+            dst_ref=part(block, c, place * share, share),
+            send_sem=send0.at[c, to],
+            recv_sem=recv0.at[c, slot],
             device_id=(to, dev),
             device_id_type=MESH,
         )
 
-    @pl.loop(1, n_grp)
-    def _(t):
-        trade((grp + t) % n_grp, grp, grp).start()
-
-    local = pltpu.make_async_copy(
-        stack.at[:, pl.ds(pl.multiple_of(grp * strip, strip), strip), :],
-        block.at[pl.ds(grp * share, share)],
-        own,
-    )
-    local.start()
+    def local(c):
+        return pltpu.make_async_copy(
+            part(stack, c, 0, share, grp), part(block, c, grp * share, share), own.at[c]
+        )
+
+    for c in range(pieces):
+
+        @pl.loop(1, n_grp)
+        def _(t):
+            trade(c, (grp + t) % n_grp, grp, grp).start()
+
+        local(c).start()
 
     inverse(solved, network, design_t, matrix, pinv)
 
-    def widen(src):
-        piece = block[pl.ds(src * share, share)].astype(jnp.float32)
+    step = lax.broadcasted_iota(jnp.int32, (strip, half), 1) // BAND - (BAND - 1)
+    row_cos, row_sin = waves(grp * strip, step.shape, step, rows_all)
+    row_wave[:, :half] = row_cos
+    row_wave[:, half:] = row_sin
+    for c in range(pieces):
+        step = lax.broadcasted_iota(jnp.int32, (LANES, half), 1) % BAND
+        col_cos, col_sin = waves(dev * items + c * LANES, step.shape, step, cols_all)
+
+        @pl.loop(0, pairs)
+        def _(q):
+            for e in range(2):
+                row = row_wave[pl.ds(q * 2 + e, 1), :]
+                row_cos, row_sin = row[:, :half], row[:, half:]
+                cos = split(row_cos * col_cos - row_sin * col_sin)
+                sin = split(row_sin * col_cos + row_cos * col_sin)
+                at = pl.ds(e * LANES, LANES)
+                for ref, i in ((high, 0), (low, 1)):
+                    ref[c * pairs + q, at, :half] = cos[i]
+                    ref[c * pairs + q, at, half:] = sin[i]
+
+    acc[...] = jnp.zeros_like(acc)
+
+    def widen(c, src):
+        piece = block[pl.ds(src * share, share), :, c * LANES : (c + 1) * LANES]
         start = pl.multiple_of(src * share * strip, strip)
-        piece = piece.reshape(share * strip, items)
-        for c in range(items // LANES):
-            data[c, pl.ds(start, share * strip), :] = piece[:, c * LANES : (c + 1) * LANES]
-
-    local.wait()
-    widen(grp)
-
-    @pl.loop(1, n_grp)
-    def _(t):
-        src = (grp + n_grp - t) % n_grp
-        trade(src, src, src).wait_recv()
-        widen(src)
-
-    acc[...] = jnp.zeros_like(acc)
-
-    @pl.loop(0, strip)
-    def _(h):
-        phase = jnp.concatenate(
-            [data[c, pl.ds(h, ifgs, stride=strip), :] for c in range(items // LANES)], axis=1
-        )
-        out = jnp.dot(pinv[...], phase.astype(jnp.bfloat16), preferred_element_type=jnp.float32)
-        series[h] = out
-        model = lax.dot_general(
-            design_t[0 : out.shape[0], :],
-            out.astype(jnp.bfloat16),
-            (((0,), (0,)), ((), ())),
-            preferred_element_type=jnp.float32,
-        )
-        resid = phase - model
-        mean = jnp.sum(resid * resid, axis=0, keepdims=True) * (1.0 / ifgs)
-        fitted[pl.ds(h, 1), :] = jnp.sqrt(mean + 1e-06)
-        acc[...] += dot3(out, basis(row_wave[pl.ds(h, 1), :], col_wave[...]), ((1,), (0,)))
+        piece = piece.astype(jnp.float32).reshape(share * strip, LANES)
+        data[c, pl.ds(start, share * strip), :] = piece
+
+    for c in range(pieces):
+        local(c).wait()
+        widen(c, grp)
+
+        @pl.loop(1, n_grp)
+        def _(t):
+            src = (grp + n_grp - t) % n_grp
+            trade(c, src, src, src).wait_recv()
+            widen(c, src)
+
+        @pl.loop(0, pairs)
+        def _(q):
+            g = c * pairs + q
+            phase = jnp.concatenate(
+                [data[c, pl.ds(q * 2 + e, ifgs, stride=strip), :] for e in range(2)], axis=1
+            )
+            out = jnp.dot(
+                pinv[...], phase.astype(jnp.bfloat16), preferred_element_type=jnp.float32
+            )
+            series[g] = out
+            model = lax.dot_general(
+                design_t[0:tall, :],
+                out.astype(jnp.bfloat16),
+                (((0,), (0,)), ((), ())),
+                preferred_element_type=jnp.float32,
+            )
+            resid = phase - model
+            mean = jnp.sum(resid * resid, axis=0, keepdims=True) * (1.0 / ifgs)
+            value = jnp.sqrt(mean + 1e-06)
+            for e in range(2):
+                fit[c, pl.ds(q * 2 + e, 1), :] = value[:, e * LANES : (e + 1) * LANES]
+            acc[...] += dot3(split(out), (high[g], low[g]), ((1,), (0,)))
+
+        fitted[:, c * LANES : (c + 1) * LANES] = fit[c]
 
     for j in range(owners):
         x[j] = acc[j * per : (j + 1) * per, :]
@@ -273,32 +295,41 @@
     lane = lax.broadcasted_iota(jnp.int32, coef.shape, 1) % (2 * BAND * BAND)
     row_step = jnp.abs(lane // BAND - (BAND - 1))
     col_step = lane % BAND
-    keep = (row_step < bands[...]) & (col_step < bands[...])
+    date = lax.broadcasted_iota(jnp.int32, (tall, solved), 0)
+    same = date == lax.broadcasted_iota(jnp.int32, (tall, solved), 1)
+    band = jnp.where(same, bands[...].astype(jnp.float32), 0.0)
+    band = jnp.sum(band, axis=1, keepdims=True)
+    keep = jnp.maximum(row_step, col_step).astype(jnp.float32) < band
     value = jnp.where(keep, coef[...] * scale, 0.0)
-    coef[...] = jnp.where(col_step > 0, value + value, value)
-    total = None
-    for piece in split3(value):
-        term = lax.dot_general(
-            choose[...], piece, (((1,), (1,)), ((), ())), preferred_element_type=jnp.float32
-        )
-        total = term if total is None else total + term
-    spectrum[...] = total[:, :solved]
-
-    @pl.loop(0, strip)
-    def _(h):
-        ramp = dot3(coef[...], basis(row_wave[pl.ds(h, 1), :], col_wave[...]), ((1,), (1,)))
-        rest = series[h] - ramp
-        for c in range(items // LANES):
-            piece = rest[:, c * LANES : (c + 1) * LANES]
-            flat[c, pl.ds(h, coef.shape[0], stride=strip), :] = piece
-
-    for c in range(items // LANES):
+    weighted = split(jnp.where(col_step > 0, value + value, value))
+    parts = split3(value)
+    for i in range(2):
+        total = None
+        for piece in parts:
+            term = lax.dot_general(
+                choose[i], piece, (((1,), (1,)), ((), ())), preferred_element_type=jnp.float32
+            )
+            total = term if total is None else total + term
+        spectrum[i] = total[:, :solved]
+
+    for c in range(pieces):
+
+        @pl.loop(0, pairs)
+        def _(q):
+            g = c * pairs + q
+            rest = series[g] - dot3(weighted, (high[g], low[g]), ((1,), (1,)))
+            for e in range(2):
+                piece = rest[:, e * LANES : (e + 1) * LANES]
+                flat[c, pl.ds(q * 2 + e, tall, stride=strip), :] = piece
+
         piece = flat[c, 0 : solved * strip, :].reshape(solved, strip, LANES)
         deramped[:, :, c * LANES : (c + 1) * LANES] = piece.astype(jnp.bfloat16)
 
-    @pl.loop(1, n_grp)
-    def _(t):
-        trade((grp + t) % n_grp, grp, grp).wait_send()
+    for c in range(pieces):
+
+        @pl.loop(1, n_grp)
+        def _(t):
+            trade(c, (grp + t) % n_grp, grp, grp).wait_send()
 
     @pl.loop(1, count)
     def _(t):
@@ -316,16 +347,16 @@
 def choice():
     freqs = 2 * BAND - 1
     half = 2 * BAND * BAND
-    table = np.zeros((freqs, freqs, 2, 2 * half), np.float32)
+    table = np.zeros((2, freqs, freqs, 2 * half), np.float32)
     for k in range(freqs):
         for m in range(freqs):
             if m >= BAND - 1:
                 at, sign = k * BAND + m - (BAND - 1), -1.0
             else:
                 at, sign = (freqs - 1 - k) * BAND + (BAND - 1) - m, 1.0
-            table[k, m, 0, at] = 1.0
-            table[k, m, 1, half + at] = sign
-    return jnp.asarray(table.reshape(-1, 2 * half), jnp.bfloat16)
+            table[0, k, m, at] = 1.0
+            table[1, k, m, half + at] = sign
+    return jnp.asarray(table.reshape(2, -1, 2 * half), jnp.bfloat16)
 
 
 def on_device(stack, network, bands):
@@ -341,22 +372,19 @@
     owners = -(-solved // per)
     tall = -(-max(solved, owners * per) // 8) * 8
     wide = -(-tall // 128) * 128
-    row_pos = lax.axis_index("grp") * strip + jnp.arange(strip, dtype=jnp.int32)
-    col_pos = lax.axis_index("dev") * items + jnp.arange(items, dtype=jnp.int32)
-    row_wave, col_wave = wave_tables(row_pos, rows_all, col_pos, cols_all)
-    bands = jnp.pad(bands, (0, tall - solved))[:, None]
-
     vmem = pl.BlockSpec(memory_space=pltpu.VMEM)
     f32, bf16 = jnp.float32, jnp.bfloat16
-    sems = lambda n: pltpu.SemaphoreType.DMA((n,))
+    sems = lambda *n: pltpu.SemaphoreType.DMA(n)
+    pieces = items // LANES
+    groups = pieces * strip // 2
     deramped, fitted, spectrum = pl.pallas_call(
         functools.partial(kernel, n_grp, n_dev, solved, 1.0 / (rows_all * cols_all)),
         out_shape=(
             jax.ShapeDtypeStruct((solved, strip, items), bf16),
             jax.ShapeDtypeStruct((strip, items), f32),
-            jax.ShapeDtypeStruct((2 * freqs * freqs, solved), f32),
+            jax.ShapeDtypeStruct((2, freqs * freqs, solved), f32),
         ),
-        in_specs=[pl.BlockSpec(memory_space=pl.ANY)] + [vmem] * 5,
+        in_specs=[pl.BlockSpec(memory_space=pl.ANY)] + [vmem] * 3,
         out_specs=(vmem, vmem, vmem),
         scratch_shapes=[
             pltpu.VMEM((ifgs, strip, items), bf16),
@@ -364,16 +392,20 @@
             pltpu.VMEM((wide, ifgs), bf16),
             pltpu.VMEM((tall, wide), f32),
             pltpu.VMEM((tall, ifgs), bf16),
-            pltpu.VMEM((strip, tall, items), f32),
+            pltpu.VMEM((groups, tall, 2 * LANES), f32),
             pltpu.VMEM((tall, lanes), f32),
             pltpu.VMEM((owners, per, lanes), f32),
             pltpu.VMEM((owners, per, lanes), f32),
             pltpu.VMEM((count, per, lanes), f32),
             pltpu.VMEM((tall, lanes), f32),
-            pltpu.VMEM((items // LANES, tall * strip, LANES), f32),
-            sems(n_grp),
-            sems(n_grp),
-            pltpu.SemaphoreType.DMA,
+            pltpu.VMEM((pieces, tall * strip, LANES), f32),
+            pltpu.VMEM((strip, lanes), f32),
+            pltpu.VMEM((groups, 2 * LANES, lanes), bf16),
+            pltpu.VMEM((groups, 2 * LANES, lanes), bf16),
+            pltpu.VMEM((pieces, strip, LANES), f32),
+            sems(pieces, n_grp),
+            sems(pieces, n_grp),
+            sems(pieces),
             sems(count),
             sems(count),
             sems(count),
@@ -381,8 +413,9 @@
         ],
         compiler_params=pltpu.CompilerParams(collective_id=0, has_side_effects=True),
         name="whole",
-    )(stack, network.T, bands, row_wave, col_wave, choice())
-    spectrum = spectrum.reshape(freqs, freqs, 2, solved).transpose(2, 3, 0, 1)
+    )(stack, network.T, bands[None, :], choice())
+    spectrum = spectrum.transpose(1, 0, 2).reshape(freqs, freqs, 2, solved)
+    spectrum = spectrum.transpose(2, 3, 0, 1)
     return (deramped, fitted, spectrum)
 
 

time: 97.7 us -> 92.8 us (0.950)
  other arithmetic: 2.05 us -> 0 us
  local copies, waits for them, and re-layouts: 6.72 us -> 5.26 us
  Pallas kernels: 88 us -> 86.7 us
    reshape x1 -> x0, local copies, waits for them, and re-layouts: 2.06 us -> none  [on_device(): spectrum = spectrum.reshape(freqs, freqs, 2, solved).transpose(2, 3, 0, 1)]
    transpose x0 -> x1, local copies, waits for them, and re-layouts: none -> 2.03 us  [on_device(): spectrum = spectrum.transpose(1, 0, 2).reshape(freqs, freqs, 2, solved)]
    concatenate x2 -> x0, other arithmetic: 1.33 us -> none  [waves(): return jnp.concatenate([jnp.cos(angle), jnp.sin(angle)], axis=1)]
    pallas_call x1, Pallas kernels: 88 us -> 86.7 us  [on_device(): pl.pallas_call(functools.partial(kernel, n_grp, n_dev, solved, 1.0 / (row...]
where the time goes in v3:
time: 92.8 us; the launch traced here: 92.6 us
  Pallas kernels  86.7 us (93%)
  local copies, waits for them, and re-layouts  5.26 us (6%)
    pallas_call x1, Pallas kernels, on_device(): pl.pallas_call(functools.partial(kernel, n_grp, n_dev, solved, 1.0 / (row...  86.7 us
    unnamed x2, local copies, waits for them, and re-layouts  3.23 us
    transpose x1, local copies, waits for them, and re-layouts, on_device(): spectrum = spectrum.transpose(1, 0, 2).reshape(freqs, freqs, 2, solved)  2.03 us

profile of v3, /device:TPU:25, one launch (start us, length us, event | category | flops | bytes accessed | tf_op | source)
XLA Modules:
  0.0 92.6 jit_solution(9779917802265276901)
XLA Ops:
  0.6 86.7 %whole.1 = (bf16[149,8,256]{2,1,0:T(8,128)(2,1)}, f32[8,256]{1,0:T(8,128)}, f32[2,225,149]{2,1,0:T(8,128)}) custom-call(bf16[38,128,256]{2,1,0:T(8,128)(2,1)} %stack.1, s32[2,608]{1,0:T(2,128)} %bitcast.8, s32[1,149]{1,0:T(1,128)} %bitcast.9, bf16[2,225,256]{2,1,0:T(8,128)(2,1)} %constant.2.clone.choose), custom_call_target="tpu_custom_call" | custom-call | tf_op jit(solution)/shard_map/whole/pallas_call | solution.py:380
  87.3 2.0 %copy.8 = f32[225,2,149]{2,1,0:T(2,128)} copy(f32[225,2,149]{2,0,1:T(8,128)} %bitcast.6) | data formatting | bytes 536400 | tf_op jit(solution)/shard_map/transpose | solution.py:417
  89.4 1.9 %copy.11 = bf16[149,8,256]{2,1,0:T(8,128)(2,1)} copy(bf16[149,8,256]{2,1,0:T(8,128)(2,1)} %get-tuple-element.12) | data formatting | bytes 1220608
  91.3 1.3 %copy.12 = f32[8,256]{1,0:T(8,128)} copy(f32[8,256]{1,0:T(8,128)} %get-tuple-element.13) | data formatting | bytes 16384

commit v4 on v3

--- a/solution.py
+++ b/solution.py
@@ -115,14 +115,14 @@
     rows_all, cols_all = strip * n_grp, items * n_dev
 
     def coords(d):
-        return (d // n_dev, d % n_dev)
+        return (lax.div(d, n_dev), lax.rem(d, n_dev))
 
     barrier = pltpu.get_barrier_semaphore()
 
     @pl.loop(1, count)
     def _(t):
         pl.semaphore_signal(
-            barrier, inc=1, device_id=coords((me + t) % count), device_id_type=MESH
+            barrier, inc=1, device_id=coords(lax.rem(me + t, count)), device_id_type=MESH
         )
 
     pl.semaphore_wait(barrier, count - 1)
@@ -246,7 +246,7 @@
 
     @pl.loop(1, count)
     def _(t):
-        dst = (me + t) % count
+        dst = lax.rem(me + t, count)
 
         @pl.when(dst < owners)
         def _():
@@ -254,37 +254,37 @@
 
     @pl.when(me < owners)
     def _():
-        y[me] = x[me]
+        got[me] = x[me]
+
+        @pl.loop(0, count, unroll=4)
+        def _(src):
+            @pl.when(src != me)
+            def _():
+                pltpu.make_async_remote_copy(
+                    src_ref=x.at[0],
+                    dst_ref=got.at[src],
+                    send_sem=send1.at[src],
+                    recv_sem=recv1.at[src],
+                    device_id=(grp, dev),
+                    device_id_type=MESH,
+                ).wait_recv()
+
+        y[me] = jnp.sum(got[...], axis=0)
 
         @pl.loop(1, count)
         def _(t):
-            src = (me + count - t) % count
-            pltpu.make_async_remote_copy(
-                src_ref=x.at[0],
-                dst_ref=got.at[src],
-                send_sem=send1.at[src],
-                recv_sem=recv1.at[src],
-                device_id=coords(src),
-                device_id_type=MESH,
-            ).wait_recv()
-            y[me] += got[src]
-
-        @pl.loop(1, count)
-        def _(t):
-            gather((me + t) % count).start()
-
-    @pl.loop(1, count)
-    def _(t):
-        src = (me + count - t) % count
-
-        @pl.when(src < owners)
+            gather(lax.rem(me + t, count)).start()
+
+    @pl.loop(0, owners)
+    def _(src):
+        @pl.when(src != me)
         def _():
             pltpu.make_async_remote_copy(
                 src_ref=y.at[0],
                 dst_ref=y.at[src],
                 send_sem=send2.at[src],
                 recv_sem=recv2.at[src],
-                device_id=coords(src),
+                device_id=(grp, dev),
                 device_id_type=MESH,
             ).wait_recv()
 
@@ -333,7 +333,7 @@
 
     @pl.loop(1, count)
     def _(t):
-        dst = (me + t) % count
+        dst = lax.rem(me + t, count)
 
         @pl.when(dst < owners)
         def _():

time: 92.8 us -> 92.6 us (level)
  no operation moved by 1% of the time
where the time goes in v4:
time: 92.6 us; the launch traced here: 92.4 us
  Pallas kernels  86.5 us (93%)
  local copies, waits for them, and re-layouts  5.26 us (6%)
    pallas_call x1, Pallas kernels, on_device(): pl.pallas_call(functools.partial(kernel, n_grp, n_dev, solved, 1.0 / (row...  86.5 us
    unnamed x2, local copies, waits for them, and re-layouts  3.23 us
    transpose x1, local copies, waits for them, and re-layouts, on_device(): spectrum = spectrum.transpose(1, 0, 2).reshape(freqs, freqs, 2, solved)  2.03 us

profile of v4, /device:TPU:25, one launch (start us, length us, event | category | flops | bytes accessed | tf_op | source)
XLA Modules:
  0.0 92.4 jit_solution(16835902197676544626)
XLA Ops:
  0.6 86.5 %whole.1 = (bf16[149,8,256]{2,1,0:T(8,128)(2,1)}, f32[8,256]{1,0:T(8,128)}, f32[2,225,149]{2,1,0:T(8,128)}) custom-call(bf16[38,128,256]{2,1,0:T(8,128)(2,1)} %stack.1, s32[2,608]{1,0:T(2,128)} %bitcast.8, s32[1,149]{1,0:T(1,128)} %bitcast.9, bf16[2,225,256]{2,1,0:T(8,128)(2,1)} %constant.2.clone.choose), custom_call_target="tpu_custom_call" | custom-call | tf_op jit(solution)/shard_map/whole/pallas_call | solution.py:380
  87.1 2.0 %copy.8 = f32[225,2,149]{2,1,0:T(2,128)} copy(f32[225,2,149]{2,0,1:T(8,128)} %bitcast.6) | data formatting | bytes 536400 | tf_op jit(solution)/shard_map/transpose | solution.py:417
  89.1 1.9 %copy.11 = bf16[149,8,256]{2,1,0:T(8,128)(2,1)} copy(bf16[149,8,256]{2,1,0:T(8,128)(2,1)} %get-tuple-element.12) | data formatting | bytes 1220608
  91.1 1.3 %copy.12 = f32[8,256]{1,0:T(8,128)} copy(f32[8,256]{1,0:T(8,128)} %get-tuple-element.13) | data formatting | bytes 16384
